TPU v7x, 128 devices: a whole 4x4x4 slice. The times are simulated.
128 devices in a mesh: grp: 16 (over z, x), ep: 8 (over y, core).
Axes of the slice: x: 4, y: 4, z: 4, core: 2. Of those that a mesh axis runs over, the one named last changes fastest.
Arguments:
- tokens: bfloat16 [256, 7168], P(('grp', 'ep')), may hold values from -6 to 6
- expert_ids: int32 [256, 8], P(('grp', 'ep')), may hold values from 0 to 15, all different within a row; in each aligned block of 2 rows (0 to 1, 2 to 3, ...) at most 2 rows name the same one
- gate_ints: int32 [256, 8], P(('grp', 'ep')), may hold values from 1 to 16
- w_gate: bfloat16 [16, 7168, 2048], P('grp', None, 'ep'), may hold values from -0.0625 to 0.0625
- w_up: bfloat16 [16, 7168, 2048], P('grp', None, 'ep'), may hold values from -0.0625 to 0.0625
- w_down: bfloat16 [16, 2048, 7168], P('grp', 'ep'), may hold values from -0.125 to 0.125
Outputs:
- mixed: bfloat16 [256, 7168], P(('grp', 'ep'))
Inputs may be any that keep to these rules, and one draw needn't show every extreme that they name: `expert_ids`: each row names 8 different experts. Within the 2 rows of one device no expert is named more than 2 times, a bound that some block reaches on some device in every draw.
All inputs are finite; a program needn't handle non-finite values.
Results may differ from a plain program's by a relative error of at most 0.015.
Values may be sent and summed in bfloat16 or wider, within the bound.
No kernel may reach another device: no remote copies, remote signals or barrier semaphores. Data moves between devices by JAX's collectives and lax.ppermute only.
A program may use at most 64 MiB of HBM per device.

v0:
```python
import jax
import jax.numpy as jnp
from jax import lax
from jax.sharding import PartitionSpec as P


def local(tokens, expert_ids, gate_ints, w_gate, w_up, w_down):
    groups = lax.axis_size("grp")
    tok_rows, width = tokens.shape
    picks = expert_ids.shape[1]
    capacity = min(tok_rows, max(2, 3 * tok_rows * picks // (2 * groups)))
    routes = expert_ids.reshape(-1)
    onehot = (routes[:, None] == jnp.arange(groups, dtype=jnp.int32)[None, :]).astype(jnp.int32)
    earlier = jnp.cumsum(onehot, axis=0) - onehot
    slots = jnp.sum(earlier * onehot, axis=1)
    position = routes * capacity + slots
    token_index = jnp.arange(tok_rows * picks, dtype=jnp.int32) // picks
    table = jnp.zeros((groups * capacity,), jnp.int32).at[position].set(token_index)
    filled = jnp.zeros((groups * capacity,), jnp.bfloat16).at[position].set(1.0)
    dispatch = (tokens[table] * filled[:, None]).reshape(groups, capacity, width)
    gate_w = w_gate[0]
    up_w = w_up[0]
    down_w = w_down[0]
    arrived = lax.all_to_all(dispatch, "grp", split_axis=0, concat_axis=0, tiled=True)
    arrived = arrived.reshape(groups * capacity, width)
    rows = lax.all_gather(arrived, "ep", axis=0, tiled=True)
    gate = jnp.dot(rows, gate_w, preferred_element_type=jnp.float32)
    up = jnp.dot(rows, up_w, preferred_element_type=jnp.float32)
    hidden = (jax.nn.silu(gate) * up).astype(jnp.bfloat16)
    summed = lax.psum_scatter(
        jnp.dot(hidden, down_w, preferred_element_type=jnp.float32).astype(jnp.bfloat16),
        "ep",
        scatter_dimension=0,
        tiled=True,
    ).astype(jnp.float32)
    summed = summed.astype(jnp.bfloat16).reshape(groups, capacity, width)
    expert_out = lax.all_to_all(summed, "grp", split_axis=0, concat_axis=0, tiled=True)
    flat_out = expert_out.reshape(groups * capacity, width)
    picked = flat_out[position].astype(jnp.float32)
    scores = gate_ints.astype(jnp.float32)
    weight = scores / jnp.sum(scores, axis=1, keepdims=True)
    mixed = jnp.sum(picked.reshape(tok_rows, picks, width) * weight[:, :, None], axis=1)
    return mixed.astype(jnp.bfloat16)


def solution(mesh):
    in_specs = (
        P(("grp", "ep"), None),
        P(("grp", "ep"), None),
        P(("grp", "ep"), None),
        P("grp", None, "ep"),
        P("grp", None, "ep"),
        P("grp", "ep", None),
    )
    out_specs = P(("grp", "ep"), None)
    return jax.shard_map(local, mesh=mesh, in_specs=in_specs, out_specs=out_specs, check_vma=False)
```

profile of v0, /device:TPU:0, one launch (start us, length us, event | category | flops | bytes accessed | tf_op | source)
XLA Modules:
  0.0 137.2 jit_solution(14040806807213435363)
XLA Ops:
  6.5 0.0 copy-start
  6.5 0.0 all-gather.2.cloned.1.call-start
  6.5 0.8 eq.15
  7.3 0.7 broadcast_multiply_fusion.1
  8.0 0.1 fusion.20
  8.1 0.2 select_reduce_fusion
  8.3 0.1 mul.43
  8.4 0.6 scatter_custom_fusion
  9.0 0.0 copy-done
  9.0 0.8 gather_fusion
  9.9 0.2 gather.9
  10.1 0.7 scatter_custom_fusion.1
  10.7 0.1 mul.45
  10.8 0.5 broadcast_multiply_fusion
  11.3 18.6 %all_to_all.10 = bf16[16,2,7168]{2,1,0:T(2,128)(2,1)S(1)} all-to-all(bf16[16,2,7168]{2,1,0:T(2,128)(2,1)S(1)} %broadcast_multiply_fusion), channel_id=1, replica_groups=mesh['grp'=16,'ep'=8] {'grp'}, dimensions={0} | all-to-all | bytes 917504 | tf_op jit(solution)/shard_map/all_to_all | solution.py:24
  29.9 0.9 reshape.53
  30.8 0.0 all-gather.2.cloned.1.call-update
  30.9 0.0 reduce-scatter.2.cloned.1.call-start
  30.9 27.6 %all-gather.2.cloned.1.call-done = bf16[256,7168]{1,0:T(8,128)(2,1)} async-done(((bf16[32,7168]{1,0:T(8,128)(2,1)}), bf16[256,7168]{1,0:T(8,128)(2,1)}) %all-gather.2.cloned.1.call-update) | async-done | bytes 3670032 | tf_op jit(solution)/shard_map/all_gather | solution.py:26
  58.5 4.3 %fusion.3 = f32[256,256]{1,0:T(8,128)S(1)} fusion(bf16[256,7168]{1,0:T(8,128)(2,1)} %all-gather.2.cloned.1.call-done, bf16[1,7168,256]{2,1,0:T(8,128)(2,1)} %param.9), kind=kOutput, calls=%fused_computation.8 | convolution fusion | flops 939524096 | bytes 7602176 | tf_op jit(solution)/shard_map/dot_general | solution.py:27
  62.8 10.0 %convolution_convert_fusion = bf16[256,7168]{1,0:T(8,128)(2,1)} fusion(bf16[1,256,7168]{2,1,0:T(8,128)(2,1)} %param.11, bf16[256,7168]{1,0:T(8,128)(2,1)} %all-gather.2.cloned.1.call-done, bf16[1,7168,256]{2,1,0:T(8,128)(2,1)} %param.10, f32[256,256]{1,0:T(8,128)S(1)} %fusion.3), kind=kOutput, calls=%fused_computation.4 | convolution fusion | flops 1881276416 | bytes 14942208 | tf_op jit(solution)/shard_map/dot_general | solution.py:31
  72.9 0.0 reduce-scatter.2.cloned.1.call-update
  72.9 37.0 %reduce-scatter.2.cloned.1.call-done = bf16[32,7168]{1,0:T(8,128)(2,1)} async-done(((bf16[256,7168]{1,0:T(8,128)(2,1)}), bf16[32,7168]{1,0:T(8,128)(2,1)}) %reduce-scatter.2.cloned.1.call-update) | async-done | bytes 458768 | tf_op jit(solution)/shard_map/reduce_scatter | solution.py:30
  109.9 2.0 %reshape.54 = bf16[16,2,7168]{2,1,0:T(2,128)(2,1)} reshape(bf16[32,7168]{1,0:T(8,128)(2,1)} %reduce-scatter.2.cloned.1.call-done) | data formatting | bytes 917504 | tf_op jit(solution)/shard_map/reshape | solution.py:36
  111.9 6.9 %all-to-all-start.1 = ((bf16[16,2,7168]{2,1,0:T(2,128)(2,1)}), bf16[16,2,7168]{2,1,0:T(2,128)(2,1)S(1)}, u32[]{:S(2)}, u32[]{:S(2)}) async-start(bf16[16,2,7168]{2,1,0:T(2,128)(2,1)} %reshape.54), calls=%async_computation.2 | async-start | bytes 917504 | tf_op jit(solution)/shard_map/all_to_all | solution.py:37
  118.8 0.0 copy-done.1
  118.8 0.1 convert_reduce_fusion
  119.0 0.1 convert_divide_fusion
  119.0 9.5 %all-to-all-done.1 = bf16[16,2,7168]{2,1,0:T(2,128)(2,1)S(1)} async-done(((bf16[16,2,7168]{2,1,0:T(2,128)(2,1)}), bf16[16,2,7168]{2,1,0:T(2,128)(2,1)S(1)}, u32[]{:S(2)}, u32[]{:S(2)}) %all-to-all-start.1) | async-done | bytes 458784 | tf_op jit(solution)/shard_map/all_to_all | solution.py:37
  128.6 0.2 reshape.55
  128.8 0.7 gather_fusion.1
  129.4 0.9 fusion.13
  (8 shorter events, 0.1 us)
Async XLA Ops:
  6.5 2.5 %copy-start = (bf16[2,7168]{1,0:T(2,128)(2,1)S(1)}, bf16[2,7168]{1,0:T(2,128)(2,1)}, u32[]{:S(2)}) copy-start(bf16[2,7168]{1,0:T(2,128)(2,1)} %param.6) | copy-start | bytes 86020
  6.5 52.0 %all-gather.2.cloned.1.call-start = ((), (), s32[]{:S(2)}) async-start(), calls=%async_computation.3 | async-start | bytes 4128768 | tf_op jit(solution)/shard_map/all_gather | solution.py:26
  30.9 79.1 %reduce-scatter.2.cloned.1.call-start = ((), (), s32[]{:S(2)}) async-start(), calls=%async_computation.4 | async-start | bytes 4128768 | tf_op jit(solution)/shard_map/reduce_scatter | solution.py:30
  72.9 46.0 %copy-start.1 = (s32[2,8]{1,0:T(2,128)S(1)}, s32[2,8]{1,0:T(2,128)}, u32[]{:S(2)}) copy-start(s32[2,8]{1,0:T(2,128)} %param.8) | copy-start | bytes 196
  111.9 16.7 %all-to-all-start.1 = ((bf16[16,2,7168]{2,1,0:T(2,128)(2,1)}), bf16[16,2,7168]{2,1,0:T(2,128)(2,1)S(1)}, u32[]{:S(2)}, u32[]{:S(2)}) async-start(bf16[16,2,7168]{2,1,0:T(2,128)(2,1)} %reshape.54), calls=%async_computation.2 | async-start | bytes 917504 | tf_op jit(solution)/shard_map/all_to_all | solution.py:37
Sparse Core Ops, SparseCore 0:
  31.0 27.5 all-gather.1
  73.0 36.8 reduce-scatter.1
where the time goes:
time: 138 us; the launch traced here: 137 us
  waiting for transfers between devices  74.2 us (54%)
  blocking collectives  18.6 us (13%)
  matrix products  14.3 us (10%)
  between operations  13.5 us (10%)
  local copies, waits for them, and re-layouts  7 us (5%)
  starting transfers between devices  6.99 us (5%)
  other arithmetic  2.53 us (2%)
    reduce_scatter x1, waiting for transfers between devices, local(): lax.psum_scatter(jnp.dot(hidden, down_w, preferred_element_type=jnp.float...  37 us
    all_gather x1, waiting for transfers between devices, local(): rows = lax.all_gather(arrived, 'ep', axis=0, tiled=True)  27.6 us
    all_to_all x1, blocking collectives, local(): lax.all_to_all(dispatch, 'grp', split_axis=0, concat_axis=0, tiled=True)  18.6 us
    dot_general x1, matrix products, local(): jnp.dot(hidden, down_w, preferred_element_type=jnp.float32)  10 us
    all_to_all x1, waiting for transfers between devices, local(): lax.all_to_all(summed, 'grp', split_axis=0, concat_axis=0, tiled=True)  9.54 us
    all_to_all x1, starting transfers between devices, local(): lax.all_to_all(summed, 'grp', split_axis=0, concat_axis=0, tiled=True)  6.95 us
    dot_general x1, matrix products, local(): gate = jnp.dot(rows, gate_w, preferred_element_type=jnp.float32)  4.26 us
  transfers between devices with their start and end apart: 3, of which 3 were waited for; matrix products, arithmetic and copies ran while one was open for 0% of the time, Pallas kernels for 0%

commit v1 on v0

v1 whole, which is shorter than its diff:
```python
import itertools

import jax
import jax.numpy as jnp
from jax import lax
from jax.experimental import pallas as pl
from jax.experimental.pallas import tpu as pltpu
from jax.sharding import Mesh
from jax.sharding import PartitionSpec as P

ALL = ("z", "x", "y", "c")
RING = 4
LANES = 128
KCH = 1024


def index(z, x, y, c):
    return ((z * RING + x) * RING + y) * 2 + c


def class_groups():
    groups = []
    for colour in range(RING):
        for c in range(2):
            members = []
            for z, y in itertools.product(range(RING), repeat=2):
                members.append(index(z, (colour + 2 * y + z) % RING, y, c))
            groups.append(members)
    return groups


def neighbour_pairs(axis, back):
    pairs = []
    for z, x, y in itertools.product(range(RING), repeat=3):
        for c in range(2):
            there = {"z": z, "x": x, "y": y}
            there[axis] = (there[axis] + (1 if c == 0 else -1)) % RING
            pair = (index(z, x, y, c), index(there["z"], there["x"], there["y"], c))
            pairs.append(pair[::-1] if back else pair)
    return pairs


def swap_pairs():
    return [(i, i ^ 1) for i in range(2 * RING**3)]


def experts_kernel(me_ref, b0, b1, b2, b3, other, wg_hbm, wu_hbm, wd_hbm, mine_ref, theirs_ref, wg, wu, wd, hid, sems):
    width = wg.shape[0]
    chunks = width // KCH
    copies = []
    for i in range(chunks):
        ks = pl.ds(i * KCH, KCH)
        pair = [
            pltpu.make_async_copy(wg_hbm.at[ks, :], wg.at[ks, :], sems.at[0, i]),
            pltpu.make_async_copy(wu_hbm.at[ks, :], wu.at[ks, :], sems.at[1, i]),
        ]
        for copy in pair:
            copy.start()
        copies.append(pair)
    down = []
    for i in range(chunks):
        ks = pl.ds(i * KCH, KCH)
        copy = pltpu.make_async_copy(wd_hbm.at[:, ks], wd.at[:, ks], sems.at[2, i])
        copy.start()
        down.append(copy)

    def rows(ks):
        return jnp.concatenate([r[:, ks] for r in (b0, b1, b2, b3, other)], axis=0)

    scores = rows(pl.ds(width, LANES)).astype(jnp.float32)
    lane = lax.broadcasted_iota(jnp.int32, scores.shape, 1)
    picked = jnp.sum(jnp.where(lane == me_ref[0], scores, 0.0), axis=1, keepdims=True)
    weight = picked / jnp.sum(scores, axis=1, keepdims=True)
    gate = up = None
    for i in range(chunks):
        ks = pl.ds(i * KCH, KCH)
        for copy in copies[i]:
            copy.wait()
        part = rows(ks)
        g = jnp.dot(part, wg[ks, :], preferred_element_type=jnp.float32)
        u = jnp.dot(part, wu[ks, :], preferred_element_type=jnp.float32)
        gate, up = (g, u) if gate is None else (gate + g, up + u)
    hid[...] = (gate / (1.0 + jnp.exp(-gate)) * up).astype(jnp.bfloat16)
    half = mine_ref.shape[0]
    for i in range(chunks):
        ks = pl.ds(i * KCH, KCH)
        down[i].wait()
        out = jnp.dot(hid[...], wd[:, ks], preferred_element_type=jnp.float32) * weight
        mine_ref[:, ks] = out[:half]
        theirs_ref[:, ks] = out[half:].astype(jnp.bfloat16)


def run_experts(me, blocks, other, wg, wu, wd):
    width, hidden = wg.shape
    rows = 2 * other.shape[0]
    half = rows // 2
    chunks = width // KCH
    vmem = pl.BlockSpec(memory_space=pltpu.VMEM)
    hbm = pl.BlockSpec(memory_space=pl.ANY)
    return pl.pallas_call(
        experts_kernel,
        out_shape=(
            jax.ShapeDtypeStruct((half, width), jnp.float32),
            jax.ShapeDtypeStruct((half, width), jnp.bfloat16),
        ),
        in_specs=[pl.BlockSpec(memory_space=pltpu.SMEM)] + [vmem] * 5 + [hbm] * 3,
        out_specs=(vmem, vmem),
        scratch_shapes=[
            pltpu.VMEM((width, hidden), jnp.bfloat16),
            pltpu.VMEM((width, hidden), jnp.bfloat16),
            pltpu.VMEM((hidden, width), jnp.bfloat16),
            pltpu.VMEM((rows, hidden), jnp.bfloat16),
            pltpu.SemaphoreType.DMA((3, chunks)),
        ],
        compiler_params=pltpu.CompilerParams(vmem_limit_bytes=48 * 1024 * 1024),
        name="experts",
    )(me, *blocks, other, wg, wu, wd)


def local(tokens, expert_ids, gate_ints, w_gate, w_up, w_down):
    width = tokens.shape[1]
    me = (lax.axis_index("z") * RING + lax.axis_index("x")).astype(jnp.int32).reshape(1)
    lane = jnp.arange(LANES, dtype=jnp.int32)
    named = expert_ids[:, :, None] == lane[None, None, :]
    scores = jnp.sum(jnp.where(named, gate_ints[:, :, None], 0), axis=1).astype(jnp.bfloat16)
    row = jnp.concatenate([tokens, scores], axis=1)
    groups = class_groups()
    n = len(groups[0])
    tiled = jnp.broadcast_to(row[None], (n, *row.shape))
    own = lax.all_to_all(tiled, ALL, split_axis=0, concat_axis=0, axis_index_groups=groups, tiled=True)
    own = own.reshape(n * row.shape[0], row.shape[1])
    blocks = [own] + [lax.ppermute(own, ALL, neighbour_pairs(a, False)) for a in "xyz"]
    other = lax.ppermute(jnp.concatenate(blocks, axis=0), ALL, swap_pairs())
    mine, theirs = run_experts(me, blocks, other, w_gate[0], w_up[0], w_down[0])
    back = lax.ppermute(theirs, ALL, swap_pairs())
    total = mine + back.astype(jnp.float32)
    size = own.shape[0]
    parts = [total[i * size:(i + 1) * size] for i in range(4)]
    acc = parts[0]
    for a, part in zip("xyz", parts[1:]):
        acc = acc + lax.ppermute(part.astype(jnp.bfloat16), ALL, neighbour_pairs(a, True)).astype(jnp.float32)
    pieces = acc.astype(jnp.bfloat16).reshape(n, tokens.shape[0], width)
    got = lax.all_to_all(pieces, ALL, split_axis=0, concat_axis=0, axis_index_groups=groups, tiled=True)
    return jnp.sum(got.astype(jnp.float32), axis=0).astype(jnp.bfloat16)


def solution(mesh):
    fine = Mesh(mesh.devices.reshape(RING, RING, RING, 2), ALL)
    in_specs = (
        P(ALL, None),
        P(ALL, None),
        P(ALL, None),
        P(("z", "x"), None, ("y", "c")),
        P(("z", "x"), None, ("y", "c")),
        P(("z", "x"), ("y", "c"), None),
    )
    return jax.shard_map(local, mesh=fine, in_specs=in_specs, out_specs=P(ALL, None), check_vma=False)
```

time: 138 us -> 87.8 us (0.64)
  waiting for transfers between devices: 74.2 us -> 22.9 us
  blocking collectives: 18.6 us -> 39.7 us
  matrix products: 14.3 us -> 0 us
  between operations: 13.5 us -> 0.07 us
  Pallas kernels: 0 us -> 9.49 us
  local copies, waits for them, and re-layouts: 7 us -> 0.69 us
  other arithmetic: 2.53 us -> 6.71 us
    reduce_scatter x1 -> x0, waiting for transfers between devices: 37 us -> none  [local(): lax.psum_scatter(jnp.dot(hidden, down_w, preferred_element_type=jnp.float...]
    all_gather x1 -> x0, waiting for transfers between devices: 27.6 us -> none  [local(): rows = lax.all_gather(arrived, 'ep', axis=0, tiled=True)]
    ppermute x0 -> x8, waiting for transfers between devices: none -> 22.9 us  [the longest x3 9.13 us: local(): lax.ppermute(own, ALL, neighbour_pairs(a, False))]
    all_to_all x1 -> x2, blocking collectives: 18.6 us -> 39.7 us  [the longest x1 22.9 us: local(): lax.all_to_all(tiled, ALL, split_axis=0, concat_axis=0, axis_index_groups...]
    dot_general x2 -> x0, matrix products: 14.3 us -> none  [the longest x1 10 us: local(): jnp.dot(hidden, down_w, preferred_element_type=jnp.float32)]
    all_to_all x1 -> x0, waiting for transfers between devices: 9.54 us -> none  [local(): lax.all_to_all(summed, 'grp', split_axis=0, concat_axis=0, tiled=True)]
    pallas_call x0 -> x1, Pallas kernels: none -> 9.49 us  [run_experts(): pl.pallas_call(experts_kernel, out_shape=(jax.ShapeDtypeStruct((half, wid...]
    ppermute x0 -> x8, starting transfers between devices: none -> 7.54 us  [the longest x3 6.36 us: local(): lax.ppermute(part.astype(jnp.bfloat16), ALL, neighbour_pairs(a, True))]
  transfers between devices with their start and end apart: 3 -> 8, of which waited for: 3 -> 8; matrix products, arithmetic and copies ran while one was open for 0% -> 0% of each run, Pallas kernels for 0% -> 0%
where the time goes in v1:
time: 87.8 us; the launch traced here: 87.1 us
  blocking collectives  39.7 us (45%)
  waiting for transfers between devices  22.9 us (26%)
  Pallas kernels  9.49 us (11%)
  starting transfers between devices  7.54 us (9%)
  other arithmetic  6.71 us (8%)
    all_to_all x1, blocking collectives, local(): lax.all_to_all(tiled, ALL, split_axis=0, concat_axis=0, axis_index_groups...  22.9 us
    all_to_all x1, blocking collectives, local(): lax.all_to_all(pieces, ALL, split_axis=0, concat_axis=0, axis_index_group...  16.8 us
    pallas_call x1, Pallas kernels, run_experts(): pl.pallas_call(experts_kernel, out_shape=(jax.ShapeDtypeStruct((half, wid...  9.49 us
    ppermute x3, waiting for transfers between devices, local(): lax.ppermute(own, ALL, neighbour_pairs(a, False))  9.13 us
    ppermute x3, starting transfers between devices, local(): lax.ppermute(part.astype(jnp.bfloat16), ALL, neighbour_pairs(a, True))  6.36 us
    ppermute x3, waiting for transfers between devices, local(): lax.ppermute(part.astype(jnp.bfloat16), ALL, neighbour_pairs(a, True))  6 us
    ppermute x1, waiting for transfers between devices, local(): other = lax.ppermute(jnp.concatenate(blocks, axis=0), ALL, swap_pairs())  4.17 us
    ppermute x1, waiting for transfers between devices, local(): back = lax.ppermute(theirs, ALL, swap_pairs())  3.65 us
  transfers between devices with their start and end apart: 8, of which 8 were waited for; matrix products, arithmetic and copies ran while one was open for 0% of the time, Pallas kernels for 0%

profile of v1, /device:TPU:0, one launch (start us, length us, event | category | flops | bytes accessed | tf_op | source)
XLA Modules:
  0.0 87.1 jit_solution(7104366596193688074)
XLA Ops:
  0.0 0.8 select_reduce_fusion
  0.8 0.8 pad_maximum_fusion.1
  1.6 0.2 broadcast_in_dim.23
  1.8 22.9 %all_to_all.10 = bf16[16,2,7296]{2,1,0:T(2,128)(2,1)S(1)} all-to-all(bf16[16,2,7296]{2,1,0:T(2,128)(2,1)S(1)} %broadcast_in_dim.23), channel_id=1, replica_groups={{0,18,4,22,40,58,44,62,80,66,84,70,120,106,124,110},{1,19,5,23,41,59,45..., dimensions={0} | all-to-all | bytes 933888 | tf_op jit(solution)/shard_map/all_to_all | solution.py:130
  24.7 0.2 reshape.13.b0
  24.9 0.1 collective-permute-start.2
  25.0 0.2 collective-permute-start.1
  25.3 0.6 collective-permute-start
  25.9 8.9 %collective-permute-done.2.b3 = bf16[32,7296]{1,0:T(8,128)(2,1)S(1)} collective-permute-done((bf16[32,7296]{1,0:T(8,128)(2,1)S(1)}, bf16[32,7296]{1,0:T(8,128)(2,1)S(1)}, u32[]{:S(2)}, u32[]{:S(2)}) %collective-permute-start.2) | collective-permute-done | bytes 466976 | tf_op jit(solution)/shard_map/ppermute | solution.py:132
  34.8 0.1 collective-permute-done.1.b2
  34.9 0.2 collective-permute-done.b1
  35.0 1.4 %pad_maximum_fusion = bf16[128,7296]{1,0:T(8,128)(2,1)} fusion(bf16[32,7296]{1,0:T(8,128)(2,1)S(1)} %collective-permute-done.2.b3, bf16[32,7296]{1,0:T(8,128)(2,1)S(1)} %collective-permute-done.1.b2, bf16[32,7296]{1,0:T(8,128)(2,1)S(1)} %collective-permute-done.b1, bf16[32,7296]{1,0:T(8,128)(2,1)S(1)} %reshape.13.b0), kind=kLoop, calls=%fused_computation.1 | loop fusion | flops 7471104 | bytes 3735552 | tf_op jit(solution)/shard_map/concatenate | solution.py:133
  36.4 0.0 collective-permute-start.3
  36.4 4.2 %collective-permute-done.3.other = bf16[128,7296]{1,0:T(8,128)(2,1)} collective-permute-done((bf16[128,7296]{1,0:T(8,128)(2,1)}, bf16[128,7296]{1,0:T(8,128)(2,1)}, u32[]{:S(2)}, u32[]{:S(2)}) %collective-permute-start.3) | collective-permute-done | bytes 1867808 | tf_op jit(solution)/shard_map/ppermute | solution.py:133
  40.6 9.5 %experts.1 = (f32[128,7168]{1,0:T(8,128)}, bf16[128,7168]{1,0:T(8,128)(2,1)S(1)}) custom-call(s32[1]{0:T(128)} %bitcast.me_ref, bf16[32,7296]{1,0:T(8,128)(2,1)S(1)} %reshape.13.b0, bf16[32,7296]{1,0:T(8,128)(2,1)S(1)} %collective-permute-done.b1, bf16[32,7296]{1,0:T(8,128)(2,1)S(1)} %collective-permute-done.1.b2, ...), custom_call_target="tpu_custom_call" | custom-call | tf_op jit(solution)/shard_map/experts/pallas_call | solution.py:100
  50.1 0.2 collective-permute-start.4
  50.3 3.7 %collective-permute-done.4 = bf16[128,7168]{1,0:T(8,128)(2,1)S(1)} collective-permute-done((bf16[128,7168]{1,0:T(8,128)(2,1)S(1)}, bf16[128,7168]{1,0:T(8,128)(2,1)S(1)}, u32[]{:S(2)}, u32[]{:S(2)}) %collective-permute-start.4) | collective-permute-done | bytes 1835040 | tf_op jit(solution)/shard_map/ppermute | solution.py:135
  54.0 2.6 %fusion.3 = (bf16[128,7168]{1,0:T(8,128)(2,1)S(1)}, f32[128,7168]{1,0:T(8,128)S(1)}) fusion(f32[128,7168]{1,0:T(8,128)} %get-tuple-element.7, bf16[128,7168]{1,0:T(8,128)(2,1)S(1)} %collective-permute-done.4), kind=kLoop, calls=%fused_computation.9 | loop fusion | flops 2752512 | bytes 11010048 | tf_op jit(solution)/shard_map/convert.3
  56.5 0.1 fusion.4
  56.6 0.4 collective-permute-start.5
  57.1 3.1 %collective-permute-start.7 = (bf16[32,7168]{1,0:T(8,128)(2,1)S(1)}, bf16[32,7168]{1,0:T(8,128)(2,1)S(1)}, u32[]{:S(2)}, u32[]{:S(2)}) collective-permute-start(bf16[32,7168]{1,0:T(8,128)(2,1)S(1)} %get-tuple-element.12), channel_id=1, source_target_pairs={{32,0},{97,1},{34,2},{99,3},{36,4},{101,5},{38,6},{103,7},{40,8},{... | collective-permute-start | bytes 1376264 | tf_op jit(solution)/shard_map/ppermute | solution.py:141
  60.2 2.8 %collective-permute-start.6 = (bf16[32,7168]{1,0:T(8,128)(2,1)S(1)}, bf16[32,7168]{1,0:T(8,128)(2,1)S(1)}, u32[]{:S(2)}, u32[]{:S(2)}) collective-permute-start(bf16[32,7168]{1,0:T(8,128)(2,1)S(1)} %get-tuple-element.13), channel_id=1, source_target_pairs={{2,0},{7,1},{4,2},{1,3},{6,4},{3,5},{0,6},{5,7},{10,8},{15,9},{12,... | collective-permute-start | bytes 1376264 | tf_op jit(solution)/shard_map/ppermute | solution.py:141
  63.0 2.2 %collective-permute-done.5 = bf16[32,7168]{1,0:T(8,128)(2,1)S(1)} collective-permute-done((bf16[32,7168]{1,0:T(8,128)(2,1)S(1)}, bf16[32,7168]{1,0:T(8,128)(2,1)S(1)}, u32[]{:S(2)}, u32[]{:S(2)}) %collective-permute-start.5) | collective-permute-done | bytes 458784 | tf_op jit(solution)/shard_map/ppermute | solution.py:141
  65.2 1.0 %collective-permute-done.7 = bf16[32,7168]{1,0:T(8,128)(2,1)S(1)} collective-permute-done((bf16[32,7168]{1,0:T(8,128)(2,1)S(1)}, bf16[32,7168]{1,0:T(8,128)(2,1)S(1)}, u32[]{:S(2)}, u32[]{:S(2)}) %collective-permute-start.7) | collective-permute-done | bytes 458784 | tf_op jit(solution)/shard_map/ppermute | solution.py:141
  66.2 2.8 %collective-permute-done.6 = bf16[32,7168]{1,0:T(8,128)(2,1)S(1)} collective-permute-done((bf16[32,7168]{1,0:T(8,128)(2,1)S(1)}, bf16[32,7168]{1,0:T(8,128)(2,1)S(1)}, u32[]{:S(2)}, u32[]{:S(2)}) %collective-permute-start.6) | collective-permute-done | bytes 458784 | tf_op jit(solution)/shard_map/ppermute | solution.py:141
  69.0 0.2 fusion.2
  69.2 0.2 reshape.14
  69.4 16.8 %all_to_all.11 = bf16[16,2,7168]{2,1,0:T(2,128)(2,1)S(1)} all-to-all(bf16[16,2,7168]{2,1,0:T(2,128)(2,1)S(1)} %reshape.14), channel_id=1, replica_groups={{0,18,4,22,40,58,44,62,80,66,84,70,120,106,124,110},{1,19,5,23,41,59,45..., dimensions={0} | all-to-all | bytes 917504 | tf_op jit(solution)/shard_map/all_to_all | solution.py:143
  86.1 1.0 %reduce_sum.22 = bf16[2,7168]{1,0:T(2,128)(2,1)} reduce(bf16[16,2,7168]{2,1,0:T(2,128)(2,1)S(1)} %all_to_all.11, bf16[]{:T(256)} %constant.15.clone.1), dimensions={0}, to_apply=%region_1.2 | reduce | flops 215040 | bytes 487426 | tf_op jit(solution)/shard_map/reduce_sum | solution.py:144
  (1 shorter events, 0.0 us)
Async XLA Ops:
  24.9 9.8 %collective-permute-start.2 = (bf16[32,7296]{1,0:T(8,128)(2,1)S(1)}, bf16[32,7296]{1,0:T(8,128)(2,1)S(1)}, u32[]{:S(2)}, u32[]{:S(2)}) collective-permute-start(bf16[32,7296]{1,0:T(8,128)(2,1)S(1)} %reshape.13.b0), channel_id=1, source_target_pairs={{0,32},{1,97},{2,34},{3,99},{4,36},{5,101},{6,38},{7,103},{8,40},{... | collective-permute-start | bytes 1400840 | tf_op jit(solution)/shard_map/ppermute | solution.py:132
  25.0 9.8 %collective-permute-start.1 = (bf16[32,7296]{1,0:T(8,128)(2,1)S(1)}, bf16[32,7296]{1,0:T(8,128)(2,1)S(1)}, u32[]{:S(2)}, u32[]{:S(2)}) collective-permute-start(bf16[32,7296]{1,0:T(8,128)(2,1)S(1)} %reshape.13.b0), channel_id=1, source_target_pairs={{0,2},{1,7},{2,4},{3,1},{4,6},{5,3},{6,0},{7,5},{8,10},{9,15},{10,... | collective-permute-start | bytes 1400840 | tf_op jit(solution)/shard_map/ppermute | solution.py:132
  25.3 9.8 %collective-permute-start = (bf16[32,7296]{1,0:T(8,128)(2,1)S(1)}, bf16[32,7296]{1,0:T(8,128)(2,1)S(1)}, u32[]{:S(2)}, u32[]{:S(2)}) collective-permute-start(bf16[32,7296]{1,0:T(8,128)(2,1)S(1)} %reshape.13.b0), channel_id=1, source_target_pairs={{0,8},{1,25},{2,10},{3,27},{4,12},{5,29},{6,14},{7,31},{8,16},{9,1... | collective-permute-start | bytes 1400840 | tf_op jit(solution)/shard_map/ppermute | solution.py:132
  36.4 4.2 %collective-permute-start.3 = (bf16[128,7296]{1,0:T(8,128)(2,1)}, bf16[128,7296]{1,0:T(8,128)(2,1)}, u32[]{:S(2)}, u32[]{:S(2)}) collective-permute-start(bf16[128,7296]{1,0:T(8,128)(2,1)} %pad_maximum_fusion), channel_id=1, source_target_pairs={{0,1},{1,0},{2,3},{3,2},{4,5},{5,4},{6,7},{7,6},{8,9},{9,8},{10,11... | collective-permute-start | bytes 5603336 | tf_op jit(solution)/shard_map/ppermute | solution.py:133
  50.1 3.9 %collective-permute-start.4 = (bf16[128,7168]{1,0:T(8,128)(2,1)S(1)}, bf16[128,7168]{1,0:T(8,128)(2,1)S(1)}, u32[]{:S(2)}, u32[]{:S(2)}) collective-permute-start(bf16[128,7168]{1,0:T(8,128)(2,1)S(1)} %get-tuple-element.8), channel_id=1, source_target_pairs={{0,1},{1,0},{2,3},{3,2},{4,5},{5,4},{6,7},{7,6},{8,9},{9,8},{10,11... | collective-permute-start | bytes 5505032 | tf_op jit(solution)/shard_map/ppermute | solution.py:135
  56.6 8.5 %collective-permute-start.5 = (bf16[32,7168]{1,0:T(8,128)(2,1)S(1)}, bf16[32,7168]{1,0:T(8,128)(2,1)S(1)}, u32[]{:S(2)}, u32[]{:S(2)}) collective-permute-start(bf16[32,7168]{1,0:T(8,128)(2,1)S(1)} %get-tuple-element.11), channel_id=1, source_target_pairs={{8,0},{25,1},{10,2},{27,3},{12,4},{29,5},{14,6},{31,7},{16,8},{1,9... | collective-permute-start | bytes 1376264 | tf_op jit(solution)/shard_map/ppermute | solution.py:141
  57.1 9.1 %collective-permute-start.7 = (bf16[32,7168]{1,0:T(8,128)(2,1)S(1)}, bf16[32,7168]{1,0:T(8,128)(2,1)S(1)}, u32[]{:S(2)}, u32[]{:S(2)}) collective-permute-start(bf16[32,7168]{1,0:T(8,128)(2,1)S(1)} %get-tuple-element.12), channel_id=1, source_target_pairs={{32,0},{97,1},{34,2},{99,3},{36,4},{101,5},{38,6},{103,7},{40,8},{... | collective-permute-start | bytes 1376264 | tf_op jit(solution)/shard_map/ppermute | solution.py:141
  60.2 8.8 %collective-permute-start.6 = (bf16[32,7168]{1,0:T(8,128)(2,1)S(1)}, bf16[32,7168]{1,0:T(8,128)(2,1)S(1)}, u32[]{:S(2)}, u32[]{:S(2)}) collective-permute-start(bf16[32,7168]{1,0:T(8,128)(2,1)S(1)} %get-tuple-element.13), channel_id=1, source_target_pairs={{2,0},{7,1},{4,2},{1,3},{6,4},{3,5},{0,6},{5,7},{10,8},{15,9},{12,... | collective-permute-start | bytes 1376264 | tf_op jit(solution)/shard_map/ppermute | solution.py:141
